TPU v7x, 32 devices: a whole 2x2x4 slice. The times are simulated.
32 devices in a mesh: dp: 2 (over x), cp: 4 (over z), tp: 4 (over y, core).
Axes of the slice: x: 2, y: 2, z: 4, core: 2. Of those that a mesh axis runs over, the one named last changes fastest.
Arguments:
- x: bfloat16 [8192, 2048], P(('dp', 'cp', 'tp')), parts along dimension 0
- idx: int32 [8192, 2], P(('dp', 'cp', 'tp')), parts along dimension 0
- gates: float32 [8192, 2], P(('dp', 'cp', 'tp')), parts along dimension 0
- wq: bfloat16 [2048, 2048], P(None, 'tp')
- wk: bfloat16 [2048, 2048], P(None, 'tp')
- wv: bfloat16 [2048, 2048], P(None, 'tp')
- wo: bfloat16 [2048, 2048], P('tp')
- w1g: bfloat16 [16, 2048, 1024], P(('cp', 'tp'))
- w1u: bfloat16 [16, 2048, 1024], P(('cp', 'tp'))
- w2: bfloat16 [16, 1024, 2048], P(('cp', 'tp'))
Outputs:
- output: bfloat16 [8192, 2048], P(('dp', 'cp', 'tp')), parts along dimension 0
There are 2 independent parts. A program takes and returns all parts, laid end to end along the dimension named above; an argument that names none is the same for every part.
All inputs are finite; a program needn't handle non-finite values.
Results may differ from a plain program's by a relative error of at most 0.00999393.
Values are sent between devices in bfloat16 or wider.
A program may use at most 1 GiB of HBM per device.

v0:
```python
import jax
import jax.numpy as jnp
from jax import lax
from jax.sharding import PartitionSpec as P

HEAD_DIM = 128
NEG = -1e30


def expert_ffn(rows, wg, wu, wd):
    gg = jnp.dot(rows, wg, preferred_element_type=jnp.float32)
    uu = jnp.dot(rows, wu, preferred_element_type=jnp.float32)
    act = (jax.nn.silu(gg) * uu).astype(jnp.bfloat16)
    return jnp.dot(act, wd, preferred_element_type=jnp.float32).astype(jnp.bfloat16)


def attention_residual(x, wq, wk, wv, wo, cp):
    rank = lax.axis_index('cp')
    xs = lax.all_gather(x, 'tp', axis=0, tiled=True)
    n = xs.shape[0]
    seg = n // 2
    q = jnp.dot(xs, wq, preferred_element_type=jnp.float32).astype(jnp.bfloat16)
    k = jnp.dot(xs, wk, preferred_element_type=jnp.float32).astype(jnp.bfloat16)
    v = jnp.dot(xs, wv, preferred_element_type=jnp.float32).astype(jnp.bfloat16)
    hq = q.shape[1] // HEAD_DIM
    hkvv = k.shape[1] // HEAD_DIM
    g = hq // hkvv
    kvs = lax.all_gather(jnp.concatenate([k, v], axis=1), 'cp', axis=0)
    rows = jnp.arange(n)

    def positions(src):
        s_id = jnp.where(rows < seg, src, 2 * cp - 1 - src)
        return s_id * seg + rows % seg

    qpos = positions(rank)
    q4 = q.reshape(n, hkvv, g, HEAD_DIM)
    scale = HEAD_DIM ** -0.5
    m = jnp.full((hkvv, g, n), NEG, jnp.float32)
    l = jnp.zeros((hkvv, g, n), jnp.float32)
    acc = jnp.zeros((hkvv, g, n, HEAD_DIM), jnp.float32)
    for j in range(cp):
        kj = kvs[j, :, :hkvv * HEAD_DIM].reshape(n, hkvv, HEAD_DIM)
        vj = kvs[j, :, hkvv * HEAD_DIM:].reshape(n, hkvv, HEAD_DIM)
        mask = positions(j)[None, :] <= qpos[:, None]
        s = jnp.einsum('nkgd,mkd->kgnm', q4, kj, preferred_element_type=jnp.float32) * scale
        s = jnp.where(mask, s, NEG)
        mn = jnp.maximum(m, jnp.max(s, axis=-1))
        w = jnp.where(mask, jnp.exp(s - mn[:, :, :, None]), 0.0)
        c = jnp.exp(m - mn)
        l = l * c + jnp.sum(w, axis=-1)
        acc = acc * c[:, :, :, None] + jnp.einsum('kgnm,mkd->kgnd', w.astype(jnp.bfloat16), vj, preferred_element_type=jnp.float32)
        m = mn
    o = (acc / l[:, :, :, None]).transpose(2, 0, 1, 3).reshape(n, hq * HEAD_DIM).astype(jnp.bfloat16)
    part = jnp.dot(o, wo, preferred_element_type=jnp.float32)
    att = lax.psum_scatter(part, 'tp', scatter_dimension=0, tiled=True)
    return (x.astype(jnp.float32) + att).astype(jnp.bfloat16)


def solution(mesh):
    cp = mesh.shape['cp']
    tp = mesh.shape['tp']
    ne = cp * tp
    rows_spec = P(('dp', 'cp', 'tp'), None)
    exp_spec = P(('cp', 'tp'), None, None)

    def local(x, idx, gates, wq, wk, wv, wo, w1g, w1u, w2):
        h = attention_residual(x, wq, wk, wv, wo, cp)
        t, hd = h.shape
        kk = idx.shape[1]
        cap = 4 * t // ne
        ea = idx.reshape(-1)
        tok = jnp.arange(t * kk) // kk
        onehot = (ea[:, None] == jnp.arange(ne)[None, :]).astype(jnp.int32)
        slot = jnp.take_along_axis(jnp.cumsum(onehot, axis=0), ea[:, None], axis=1)[:, 0] - 1
        send = jnp.zeros((ne, cap, hd), jnp.bfloat16).at[ea, slot].set(h[tok])
        recv = lax.all_to_all(send, ('cp', 'tp'), 0, 0, tiled=True)
        z = expert_ffn(recv.reshape(ne * cap, hd), w1g[0], w1u[0], w2[0])
        back = lax.all_to_all(z.reshape(ne, cap, hd), ('cp', 'tp'), 0, 0, tiled=True)
        zt = back[ea, slot].astype(jnp.float32).reshape(t, kk, hd)
        y = h.astype(jnp.float32) + jnp.sum(gates[:, :, None] * zt, axis=1)
        return y.astype(jnp.bfloat16)

    return jax.shard_map(local, mesh=mesh, in_specs=(rows_spec, rows_spec, rows_spec, P(None, 'tp'), P(None, 'tp'), P(None, 'tp'), P('tp', None), exp_spec, exp_spec, exp_spec), out_specs=rows_spec, check_vma=False)
```

profile of v0, /device:TPU:15, one launch (start us, length us, event | category | flops | bytes accessed | tf_op | source)
XLA Modules:
  0.0 773.7 jit_solution(11520125448848367464)
XLA Ops:
  7.3 36.5 %all-gather.4.cloned.1.call-done = bf16[1024,2048]{1,0:T(8,128)(2,1)} async-done(((bf16[256,2048]{1,0:T(8,128)(2,1)}), bf16[1024,2048]{1,0:T(8,128)(2,1)}) %all-gather.4.cloned.1.call-update) | async-done | bytes 4194320 | tf_op jit(solution)/shard_map/all_gather | solution.py:19
  43.8 5.4 convolution_convert_fusion.1
  53.8 3.7 broadcast_compare_fusion.3
  57.5 4.0 convolution_convert_fusion
  61.6 138.7 %all-gather.6.cloned.1.call-done = bf16[4096,1024]{0,1:T(8,128)(2,1)} async-done(((bf16[1024,1024]{0,1:T(8,128)(2,1)}), bf16[4096,1024]{0,1:T(8,128)(2,1)}) %all-gather.6.cloned.1.call-update) | async-done | bytes 8388624 | tf_op jit(solution)/shard_map/all_gather | solution.py:28
  200.3 14.6 %reshape.517 = bf16[4,1024,1024]{1,0,2:T(4,128)(2,1)} reshape(bf16[4096,1024]{0,1:T(8,128)(2,1)} %all-gather.6.cloned.1.call-done) | data formatting | bytes 16777216 | tf_op jit(solution)/shard_map/all_gather | solution.py:28
  214.8 21.1 %fusion.80 = (bf16[1,1024,512]{1,0,2:T(2,128)(2,1)}, bf16[1,1024,512]{1,0,2:T(2,128)(2,1)S(1)}, bf16[1,1024,512]{1,0,2:T(2,128)(2,1)}, bf16[1,1024,512]{1,0,2:T(...) fusion(bf16[4,1024,1024]{1,0,2:T(4,128)(2,1)} %reshape.517), kind=kLoop, calls=%fused_computation.122 | loop fusion | bytes 16777216 | tf_op jit(solution)/shard_map/slice | solution.py:43
  243.1 7.7 fusion
  250.8 3.4 fusion.3
  254.3 7.5 fusion.2
  261.8 7.5 fusion.1
  270.0 12.7 %fusion.16 = f32[4,1024,128]{1,2,0:T(8,128)} fusion(bf16[1024,4,128]{0,2,1:T(8,128)(2,1)} %bitcast.160, f32[4,1024,1024]{2,1,0:T(8,128)} %get-tuple-element.35, f32[4,1024]{1,0:T(4,128)} %get-tuple-element.23, pred[1024,1024]{0,1:T(8,128)(4,1)} %get-tuple-element.24), kind=kOutput, calls=%fused_computation.28 | convolution fusion | flops 1094713344 | bytes 20987904 | tf_op jit(solution)/shard_map/kgnm,mkd->kgnd/dot_general | solution.py:51
  282.6 14.5 %fusion.4 = (f32[4,1024]{1,0:T(4,128)}, f32[4,1024]{1,0:T(4,128)}) fusion(f32[4,1024,1024]{2,1,0:T(8,128)} %get-tuple-element.35, f32[4,1024]{1,0:T(4,128)} %get-tuple-element.23, pred[1024,1024]{0,1:T(8,128)(4,1)S(1)} %copy-done.8, f32[4,1024]{1,0:T(4,128)} %get-tuple-element.11, f32[4,1024,1024]{2,1,0:T(8,128)} %get-tuple-element.33, ...), kind=kLoop, calls=%fused_computation.16 | loop fusion | flops 41934848 | bytes 35717120 | tf_op jit(solution)/shard_map/reduce_sum | solution.py:50
  297.2 12.2 %fusion.18 = f32[4,1024,128]{1,2,0:T(8,128)} fusion(bf16[1024,4,128]{0,2,1:T(8,128)(2,1)} %bitcast.158, f32[4,1024,1024]{2,1,0:T(8,128)} %get-tuple-element.33, f32[4,1024]{1,0:T(4,128)} %get-tuple-element.11, pred[1024,1024]{0,1:T(8,128)(4,1)S(1)} %copy-done.6), kind=kOutput, calls=%fused_computation.29 | convolution fusion | flops 1094713344 | bytes 20987904 | tf_op jit(solution)/shard_map/kgnm,mkd->kgnd/dot_general | solution.py:51
  309.4 3.1 copy.62
  313.9 12.3 %fusion.20 = f32[4,1024,128]{1,2,0:T(8,128)} fusion(bf16[1024,4,128]{0,2,1:T(8,128)(2,1)} %bitcast.161, f32[4,1024,1024]{2,1,0:T(8,128)} %get-tuple-element.31, f32[4,1024]{1,0:T(4,128)} %get-tuple-element.10, pred[1024,1024]{0,1:T(8,128)(4,1)S(1)} %copy-done.4), kind=kOutput, calls=%fused_computation.30 | convolution fusion | flops 1094713344 | bytes 20987904 | tf_op jit(solution)/shard_map/kgnm,mkd->kgnd/dot_general | solution.py:51
  326.2 12.1 %fusion.8 = (f32[4,1024]{1,0:T(4,128)S(1)}, f32[4,1024]{1,0:T(4,128)S(1)}) fusion(f32[4,1024,1024]{2,1,0:T(8,128)} %get-tuple-element.31, f32[4,1024]{1,0:T(4,128)} %get-tuple-element.10, pred[1024,1024]{0,1:T(8,128)(4,1)S(1)} %copy-done.4, f32[4,1024]{1,0:T(4,128)S(1)} %get-tuple-element.9, f32[4,1024,1024]{2,1,0:T(8,128)S(1)} %get-tuple-element.29, ...), kind=kLoop, calls=%fused_computation.20 | loop fusion | flops 41934848 | bytes 35717120 | tf_op jit(solution)/shard_map/reduce_sum | solution.py:50
  338.3 8.4 %divide_convert_fusion = bf16[4,1024,128]{1,2,0:T(8,128)(2,1)} fusion(f32[4,1024,128]{1,2,0:T(8,128)} %fusion.20, f32[4,1024,128]{1,2,0:T(8,128)} %fusion.18, f32[4,1024,128]{1,2,0:T(8,128)} %fusion.16, bf16[1024,4,128]{0,2,1:T(8,128)(2,1)} %bitcast.159, f32[4,1024,1024]{2,1,0:T(8,128)S(1)} %get-tuple-element.29, f32[4,1024]{1,0:T(4,128)S(1)} %get-tuple-element.9, ...), kind=kOutput, calls=%fused_computation.48 | convolution fusion | flops 1099431936 | bytes 26312704 | tf_op jit(solution)/shard_map/kgnm,mkd->kgnd/dot_general | solution.py:51
  346.7 6.8 fusion.81
  356.3 4.5 gather_fusion.2
  360.9 63.7 %reduce-scatter.2.cloned.1.call-done = f32[256,2048]{1,0:T(8,128)} async-done(((f32[1024,2048]{1,0:T(8,128)}), f32[256,2048]{1,0:T(8,128)}) %reduce-scatter.2.cloned.1.call-update) | async-done | bytes 2097168 | tf_op jit(solution)/shard_map/reduce_scatter | solution.py:55
  426.8 3.3 gather_fusion
  432.6 92.8 %scatter_fusion = bf16[16,64,2048]{2,1,0:T(8,128)(2,1)} fusion(bf16[16,64,2048]{2,1,0:T(8,128)(2,1)} %broadcast_in_dim.120, s32[512]{0:T(512)S(1)} %bitcast.149, bf16[512,2048]{1,0:T(8,128)(2,1)} %gather_fusion), kind=kCustom, calls=%fused_computation.3 | custom fusion | bytes 6295552 | tf_op jit(solution)/shard_map/scatter | solution.py:75
  525.5 99.2 %all_to_all.10 = bf16[16,64,2048]{2,1,0:T(8,128)(2,1)S(1)} all-to-all(bf16[16,64,2048]{2,1,0:T(8,128)(2,1)} %scatter_fusion), channel_id=1, replica_groups=mesh['dp'=2,'cp'=4,'tp'=4] {'cp','tp'}, dimensions={0} | all-to-all | bytes 8388608 | tf_op jit(solution)/shard_map/all_to_all | solution.py:76
  624.7 4.5 fusion.30
  629.2 5.4 multiply_convert_fusion
  634.6 6.1 fusion.34
  640.7 5.1 all-to-all-start.1
  645.9 92.4 %all-to-all-done.1 = bf16[16,64,2048]{2,1,0:T(8,128)(2,1)} async-done(((bf16[16,64,2048]{2,1,0:T(8,128)(2,1)}), bf16[16,64,2048]{2,1,0:T(8,128)(2,1)}, u32[]{:S(2)}, u32[]{:S(2)}) %all-to-all-start.1) | async-done | bytes 4194336 | tf_op jit(solution)/shard_map/all_to_all | solution.py:78
  738.3 13.0 %gather_fusion.1 = bf16[512,2048]{1,0:T(8,128)(2,1)} fusion(bf16[16,64,2048]{2,1,0:T(8,128)(2,1)} %all-to-all-done.1, s32[512]{0:T(512)S(1)} %bitcast.148), kind=kCustom, calls=%fused_computation.1 | custom fusion | bytes 4198400 | tf_op jit(solution)/shard_map/gather | solution.py:79
  751.3 5.4 reshape.488
  756.7 8.9 %multiply_reduce_fusion = f32[256,2048]{1,0:T(8,128)S(1)} fusion(f32[256,2,2048]{2,1,0:T(2,128)} %reshape.488, f32[256,2]{1,0:T(8,128)S(1)} %copy.40), kind=kLoop, calls=%fused_computation.42 | loop fusion | flops 1572864 | bytes 6293504 | tf_op jit(solution)/shard_map/reduce_sum | solution.py:80
  (93 shorter events, 23.4 us)
Async XLA Ops:
  6.5 340.2 %copy-start = (bf16[512,2048]{1,0:T(8,128)(2,1)S(1)}, bf16[512,2048]{1,0:T(8,128)(2,1)}, u32[]{:S(2)}) copy-start(bf16[512,2048]{1,0:T(8,128)(2,1)} %param.16) | copy-start | bytes 6291460
  6.5 37.2 %all-gather.4.cloned.1.call-start = ((), (), s32[]{:S(2)}) async-start(), calls=%async_computation.3 | async-start | bytes 5242880 | tf_op jit(solution)/shard_map/all_gather | solution.py:19
  7.3 193.0 %all-gather.6.cloned.1.call-start = ((), (), s32[]{:S(2)}) async-start(), calls=%async_computation.5 | async-start | bytes 10485760 | tf_op jit(solution)/shard_map/all_gather | solution.py:28
  43.8 5.4 copy-start.22
  43.8 5.4 copy-start.24
  53.2 371.5 %reduce-scatter.2.cloned.1.call-start = ((), (), s32[]{:S(2)}) async-start(), calls=%async_computation.4 | async-start | bytes 10485760 | tf_op jit(solution)/shard_map/reduce_scatter | solution.py:55
  53.7 3.8 copy-start.23
  239.0 4.1 copy-start.7
  243.1 7.7 copy-start.1
  243.1 7.7 copy-start.12
  250.8 3.4 copy-start.3
  250.8 3.4 copy-start.11
  254.2 7.6 copy-start.5
  254.2 7.5 copy-start.10
  270.0 12.7 %copy-start.6 = (pred[1024,1024]{0,1:T(8,128)(4,1)S(1)}, pred[1024,1024]{0,1:T(8,128)(4,1)}, u32[]{:S(2)}) copy-start(pred[1024,1024]{0,1:T(8,128)(4,1)} %get-tuple-element.25) | copy-start | bytes 3145732
  270.0 12.7 %copy-start.8 = (pred[1024,1024]{0,1:T(8,128)(4,1)S(1)}, pred[1024,1024]{0,1:T(8,128)(4,1)}, u32[]{:S(2)}) copy-start(pred[1024,1024]{0,1:T(8,128)(4,1)} %get-tuple-element.24) | copy-start | bytes 3145732
  309.4 3.1 copy-start.9
  309.4 4.5 copy-start.4
  313.9 12.3 %copy-start.2 = (pred[1024,1024]{0,1:T(8,128)(4,1)S(1)}, pred[1024,1024]{0,1:T(8,128)(4,1)}, u32[]{:S(2)}) copy-start(pred[1024,1024]{0,1:T(8,128)(4,1)} %get-tuple-element.27) | copy-start | bytes 3145732
  326.2 12.1 %copy-start.13 = (f32[4,1024]{1,0:T(4,128)S(1)}, f32[4,1024]{1,0:T(4,128)}, u32[]{:S(2)}) copy-start(f32[4,1024]{1,0:T(4,128)} %get-tuple-element.10) | copy-start | bytes 49156
  326.2 12.1 %copy-start.14 = (f32[4,1024]{1,0:T(4,128)S(1)}, f32[4,1024]{1,0:T(4,128)}, u32[]{:S(2)}) copy-start(f32[4,1024]{1,0:T(4,128)} %get-tuple-element.11) | copy-start | bytes 49156
  326.2 12.1 %copy-start.15 = (f32[4,1024]{1,0:T(4,128)S(1)}, f32[4,1024]{1,0:T(4,128)}, u32[]{:S(2)}) copy-start(f32[4,1024]{1,0:T(4,128)} %get-tuple-element.36) | copy-start | bytes 49156
  326.2 12.1 %copy-start.16 = (f32[4,1024]{1,0:T(4,128)S(1)}, f32[4,1024]{1,0:T(4,128)}, u32[]{:S(2)}) copy-start(f32[4,1024]{1,0:T(4,128)} %get-tuple-element.37) | copy-start | bytes 49156
  353.5 0.7 copy-start.17
  525.5 99.2 %copy-start.19 = (bf16[1,2048,1024]{2,1,0:T(8,128)(2,1)S(1)}, bf16[1,2048,1024]{2,1,0:T(8,128)(2,1)}, u32[]{:S(2)}) copy-start(bf16[1,2048,1024]{2,1,0:T(8,128)(2,1)} %param.18) | copy-start | bytes 12582916
  624.7 4.5 copy-start.20
  629.2 5.4 copy-start.21
  640.7 5.1 copy-start.18
  640.7 97.6 %all-to-all-start.1 = ((bf16[16,64,2048]{2,1,0:T(8,128)(2,1)}), bf16[16,64,2048]{2,1,0:T(8,128)(2,1)}, u32[]{:S(2)}, u32[]{:S(2)}) async-start(bf16[16,64,2048]{2,1,0:T(8,128)(2,1)} %bitcast.155), calls=%async_computation.2 | async-start | bytes 8388608 | tf_op jit(solution)/shard_map/all_to_all | solution.py:78
Sparse Core Ops, SparseCore 0:
  8.9 34.8 all-gather.3
  53.3 146.9 all-gather.5
  353.7 70.9 reduce-scatter.1
where the time goes:
time: 781 us; the launch traced here: 774 us
  waiting for transfers between devices  332 us (43%)
  local copies, waits for them, and re-layouts  171 us (22%)
  matrix products  106 us (14%)
  blocking collectives  99.2 us (13%)
  other arithmetic  46.2 us (6%)
  between operations  13.7 us (2%)
    all_gather x1, waiting for transfers between devices, attention_residual(): kvs = lax.all_gather(jnp.concatenate([k, v], axis=1), 'cp', axis=0)  139 us
    all_to_all x1, blocking collectives, local(): recv = lax.all_to_all(send, ('cp', 'tp'), 0, 0, tiled=True)  99.2 us
    scatter x1, local copies, waits for them, and re-layouts, local(): send = jnp.zeros((ne, cap, hd), jnp.bfloat16).at[ea, slot].set(h[tok])  92.8 us
    all_to_all x1, waiting for transfers between devices, local(): lax.all_to_all(z.reshape(ne, cap, hd), ('cp', 'tp'), 0, 0, tiled=True)  92.4 us
    reduce_scatter x1, waiting for transfers between devices, attention_residual(): att = lax.psum_scatter(part, 'tp', scatter_dimension=0, tiled=True)  63.7 us
    dot_general x4, matrix products, attention_residual(): jnp.einsum('kgnm,mkd->kgnd', w.astype(jnp.bfloat16), vj, preferred_elemen...  45.5 us
    all_gather x1, waiting for transfers between devices, attention_residual(): xs = lax.all_gather(x, 'tp', axis=0, tiled=True)  36.5 us
    reduce_sum x2, other arithmetic, attention_residual(): l = l * c + jnp.sum(w, axis=-1)  26.6 us
  transfers between devices with their start and end apart: 4, of which 4 were waited for; matrix products, arithmetic and copies ran while one was open for 2% of the time, Pallas kernels for 0%

commit v1 on v0

v1 whole, which is shorter than its diff:
```python
import functools

import jax
import jax.numpy as jnp
from jax import lax
from jax.experimental import pallas as pl
from jax.experimental.pallas import tpu as pltpu
from jax.sharding import PartitionSpec as P

HD = 128
BF = jnp.bfloat16
F32 = jnp.float32
MESH = pl.DeviceIdType.MESH
NEG = -1e30
ANY = pl.BlockSpec(memory_space=pl.ANY)
VM = pl.BlockSpec(memory_space=pltpu.VMEM)
MIB = 2 ** 20


def remote(src, dst, ssem, rsem, c, t):
    return pltpu.make_async_remote_copy(
        src_ref=src, dst_ref=dst, send_sem=ssem, recv_sem=rsem,
        device_id={'cp': c, 'tp': t}, device_id_type=MESH)


def group_barrier(c, t):
    sem = pltpu.get_barrier_semaphore()
    for i in range(1, 16):
        pl.semaphore_signal(sem, inc=1, device_id={'cp': c ^ (i // 4), 'tp': t ^ (i % 4)}, device_id_type=MESH)
    pl.semaphore_wait(sem, 15)


def kernel_a(x_ref, idx_ref, wq_ref, wk_ref, wv_ref, wo_ref,
             qkv_ref, woa_ref, cnt_ref,
             xs, sb, cb, xsend, xrecv, wsend, wrecv, qsend, qrecv, qloc, csend, crecv):
    c = lax.axis_index('cp')
    t = lax.axis_index('tp')
    y = t // 2
    rows = x_ref.shape[0]
    seg = 2 * rows
    nseg = 8
    e = lax.broadcasted_iota(jnp.int32, (rows, HD), 1)
    hit = (idx_ref[:, 0:1] == e).astype(F32) + (idx_ref[:, 1:2] == e).astype(F32)
    load = jnp.max(jnp.sum(hit, axis=0, keepdims=True), axis=1, keepdims=True)
    cb[...] = jnp.broadcast_to(load, cb.shape)
    me = c * 4 + t

    group_barrier(c, t)
    pending = []

    def go(cp):
        cp.start()
        pending.append(cp)

    own = pl.ds(pl.multiple_of(t * rows, rows), rows)
    go(remote(x_ref, xs.at[own], xsend.at[0], xrecv.at[t], c, t ^ 1))
    go(remote(x_ref, xs.at[own], xsend.at[1], xrecv.at[t], c, t ^ 2))
    xs[own, :] = x_ref[...]
    go(remote(wo_ref, woa_ref.at[t], wsend.at[0], wrecv.at[t], c, t ^ 1))
    go(remote(wo_ref, woa_ref.at[t], wsend.at[1], wrecv.at[t], c, t ^ 2))
    for i in range(1, 16):
        go(remote(cb, cnt_ref.at[me], csend.at[i], crecv.at[me], c ^ (i // 4), t ^ (i % 4)))
    cloc = pltpu.make_async_copy(cb, cnt_ref.at[me], csend.at[0])
    cloc.start()

    def xwait(tt):
        r = pl.ds(pl.multiple_of(tt * rows, rows), rows)
        remote(xs.at[r], xs.at[r], xsend.at[0], xrecv.at[tt], c, t ^ 1).wait_recv()

    locs = []

    def half(p, row0, s):
        for m, w in enumerate((wq_ref, wk_ref, wv_ref)):
            r = jnp.dot(xs[pl.ds(row0, seg), :], w[...], preferred_element_type=F32).astype(BF)
            for hh in range(4):
                sb[p, m, hh] = r[:, hh * HD:(hh + 1) * HD]
            dst = qkv_ref.at[m, s]
            for off in (2, 3, 1):
                c2 = c ^ off
                go(remote(sb.at[p, m, c2], dst, qsend.at[p, m, off], qrecv.at[m, s], c2, t))
            lc = pltpu.make_async_copy(sb.at[p, m, c], dst, qloc.at[p, m])
            lc.start()
            locs.append(lc)

    xwait(t ^ 1)
    half(0, pl.multiple_of(y * seg, seg), jnp.where(y == 0, c, nseg - 1 - c))
    xwait(t ^ 2)
    r2 = pl.ds(pl.multiple_of((t ^ 2) * rows, rows), rows)
    go(remote(xs.at[r2], xs.at[r2], xsend.at[2], xrecv.at[t ^ 2], c, t ^ 1))
    xwait(t ^ 3)
    half(1, pl.multiple_of((1 - y) * seg, seg), jnp.where(y == 1, c, nseg - 1 - c))

    def wwait(tt):
        remote(wo_ref, woa_ref.at[tt], wsend.at[0], wrecv.at[tt], c, t ^ 1).wait_recv()

    wwait(t ^ 2)
    go(remote(woa_ref.at[t ^ 2], woa_ref.at[t ^ 2], wsend.at[2], wrecv.at[t ^ 2], c, t ^ 1))
    wwait(t ^ 1)
    wwait(t ^ 3)
    for off in (1, 2, 3):
        c2 = c ^ off
        for s in (c2, nseg - 1 - c2):
            for m in range(3):
                remote(sb.at[0, 0, 0], qkv_ref.at[m, s], qsend.at[0, 0, 0], qrecv.at[m, s], c2, t).wait_recv()
    for i in range(1, 16):
        other = (c ^ (i // 4)) * 4 + (t ^ (i % 4))
        remote(cb, cnt_ref.at[other], csend.at[i], crecv.at[other], c ^ (i // 4), t ^ (i % 4)).wait_recv()
    for cp in pending:
        cp.wait_send()
    for lc in locs:
        lc.wait()
    cloc.wait()


def kernel_b(qkv_ref, x_ref, wo_ref, woa_ref, h_ref,
             qkv, vt, wv, acc, ob, orecv, lsem, wsem, osend, oloc, orsem):
    c = lax.axis_index('cp')
    t = lax.axis_index('tp')
    y = t // 2
    rows = x_ref.shape[0]
    seg = 2 * rows
    nseg = 8
    loads = []
    for m in range(3):
        cp = pltpu.make_async_copy(qkv_ref.at[m], qkv.at[m], lsem.at[m])
        cp.start()
        loads.append(cp)
    wl = []
    for i in range(4):
        tt = t ^ i
        cp = pltpu.make_async_copy(wo_ref if i == 0 else woa_ref.at[tt], wv.at[tt], wsem.at[i])
        cp.start()
        wl.append(cp)
    group_barrier(c, t)
    for cp in loads:
        cp.wait()
    for s in range(nseg):
        vt[:, s * seg:(s + 1) * seg] = qkv[2, s].T
    k2 = (HD ** -0.5) * 1.4426950408889634
    hcol = pl.ds(pl.multiple_of((t * 4 + c) * HD, HD), HD)
    me = c * 4 + t

    def block(s, j, diag, m, l):
        q = qkv[0, s]
        sc = lax.dot_general(qkv[1, j], q, (((1,), (1,)), ((), ())), preferred_element_type=F32)
        if diag:
            ki = lax.broadcasted_iota(jnp.int32, sc.shape, 0)
            qi = lax.broadcasted_iota(jnp.int32, sc.shape, 1)
            sc = jnp.where(ki <= qi, sc, NEG)
        mn = jnp.maximum(m, jnp.max(sc, axis=0, keepdims=True))
        w = jnp.exp2((sc - mn) * k2)
        a = jnp.exp2((m - mn) * k2)
        l = l * a + jnp.sum(w, axis=0, keepdims=True)
        vj = vt[:, pl.ds(pl.multiple_of(j * seg, seg), seg)]
        acc[...] = acc[...] * a + jnp.dot(vj, w.astype(BF), preferred_element_type=F32)
        return mn, l

    def dest(s, hf):
        low = s < 4
        return jnp.where(low, s, nseg - 1 - s), jnp.where(low, hf, 2 + hf)

    def send(s, hf):
        c2, t2 = dest(s, hf)
        src = ob.at[s, pl.ds(hf * rows, rows)]
        rm = remote(src, orecv.at[:, hcol], osend.at[s, hf], orsem.at[me], c2, t2)
        lc = pltpu.make_async_copy(src, orecv.at[:, hcol], oloc.at[0])
        return jnp.logical_and(c2 == c, t2 == t), rm, lc

    def qblock(s, _):
        acc[...] = jnp.zeros_like(acc)
        m = jnp.full((1, seg), NEG, F32)
        l = jnp.zeros((1, seg), F32)
        m, l = lax.fori_loop(0, s, lambda j, ml: block(s, j, False, *ml), (m, l))
        m, l = block(s, s, True, m, l)
        ob[s] = (acc[...] / l).T.astype(BF)
        for hf in range(2):
            mine, rm, lc = send(s, hf)

            @pl.when(jnp.logical_not(mine))
            def _():
                rm.start()

            @pl.when(mine)
            def _():
                lc.start()
        return 0

    lax.fori_loop(0, nseg, qblock, 0)
    for cp in wl:
        cp.wait()
    for i in range(1, 16):
        c2, t2 = c ^ (i // 4), t ^ (i % 4)
        hc = pl.ds(pl.multiple_of((t2 * 4 + c2) * HD, HD), HD)
        remote(ob.at[0, pl.ds(0, rows)], orecv.at[:, hc], osend.at[0, 0], orsem.at[c2 * 4 + t2], c2, t2).wait_recv()
    pltpu.make_async_copy(ob.at[0, pl.ds(0, rows)], orecv.at[:, hcol], oloc.at[0]).wait()
    for nb in range(4):
        cols = slice(nb * 512, (nb + 1) * 512)
        a = x_ref[:, cols].astype(F32)
        p = jnp.zeros_like(a)
        for tt in range(4):
            p = p + jnp.dot(orecv[:, tt * 512:(tt + 1) * 512], wv[tt, :, cols], preferred_element_type=F32)
        h_ref[:, cols] = (a + p).astype(BF)

    def drain(s, _):
        for hf in range(2):
            mine, rm, lc = send(s, hf)

            @pl.when(jnp.logical_not(mine))
            def _():
                rm.wait_send()
        return 0

    lax.fori_loop(0, nseg, drain, 0)


def kernel_c(cap, h_ref, idx_ref, idxt_ref, gates_ref, w1g_ref, w1u_ref, w2_ref, y_ref,
             wg, wu, wd, sb, rb, zb, bb, wsem, dsend, drecv, zsend, zrecv, dloc, zloc):
    c = lax.axis_index('cp')
    t = lax.axis_index('tp')
    me = c * 4 + t
    rows = h_ref.shape[0]
    ne = 16
    wl = [pltpu.make_async_copy(a.at[0], b, wsem.at[i])
          for i, (a, b) in enumerate(((w1g_ref, wg), (w1u_ref, wu), (w2_ref, wd)))]
    for cp in wl:
        cp.start()
    ei = lax.broadcasted_iota(jnp.int32, (HD, rows), 0)
    o0 = (idxt_ref[0:1, :] == ei).astype(F32)
    o1 = (idxt_ref[1:2, :] == ei).astype(F32)
    ri = lax.broadcasted_iota(jnp.int32, (rows, rows), 0)
    ci = lax.broadcasted_iota(jnp.int32, (rows, rows), 1)
    rank = jnp.dot((o0 + o1).astype(BF), (ri < ci).astype(BF), preferred_element_type=F32)
    base = ei.astype(F32) * cap + rank
    d0 = jnp.sum(o0 * base, axis=0, keepdims=True)
    d1 = jnp.sum(o1 * base, axis=0, keepdims=True)
    ki = lax.broadcasted_iota(jnp.int32, (ne * cap, rows), 0).astype(F32)
    pack = jnp.logical_or(ki == d0, ki == d1).astype(BF)
    sb[...] = jnp.dot(pack, h_ref[...], preferred_element_type=F32).astype(BF).reshape(sb.shape)
    group_barrier(c, t)
    order = [(o, i) for o in (2, 3, 1, 0) for i in range(4)]
    sends = []
    for off, i in order:
        c2, t2 = c ^ off, t ^ i
        k2 = c2 * 4 + t2
        if off == 0 and i == 0:
            own = pltpu.make_async_copy(sb.at[me], rb.at[0], dloc.at[0])
            own.start()
        else:
            cp = remote(sb.at[k2], rb.at[off * 4 + i], dsend.at[off * 4 + i], drecv.at[off * 4 + i], c2, t2)
            cp.start()
            sends.append(cp)
    for cp in wl:
        cp.wait()
    for off in (0, 2, 1, 3):
        for i in range(4):
            if off == 0 and i == 0:
                own.wait()
            else:
                remote(sb.at[0], rb.at[off * 4 + i], dsend.at[off * 4 + i], drecv.at[off * 4 + i], c ^ off, t ^ i).wait_recv()
        r = rb[off * 4:off * 4 + 4].reshape(4 * cap, -1)
        g = jnp.dot(r, wg[...], preferred_element_type=F32)
        u = jnp.dot(r, wu[...], preferred_element_type=F32)
        a = (g * jax.nn.sigmoid(g) * u).astype(BF)
        z = jnp.dot(a, wd[...], preferred_element_type=F32).astype(BF)
        zb[off * 4:off * 4 + 4] = z.reshape(4, cap, -1)
        for i in range(4):
            k = off * 4 + i
            if k == 0:
                zown = pltpu.make_async_copy(zb.at[0], bb.at[me], zloc.at[0])
                zown.start()
            else:
                cp = remote(zb.at[k], bb.at[me], zsend.at[k], zrecv.at[k], c ^ off, t ^ i)
                cp.start()
                sends.append(cp)
    ej = lax.broadcasted_iota(jnp.int32, (rows, HD), 1)
    q0 = (idx_ref[:, 0:1] == ej).astype(F32)
    q1 = (idx_ref[:, 1:2] == ej).astype(F32)
    rk = jnp.dot((ci < ri).astype(BF), (q0 + q1).astype(BF), preferred_element_type=F32)
    bs = ej.astype(F32) * cap + rk
    f0 = jnp.sum(q0 * bs, axis=1, keepdims=True)
    f1 = jnp.sum(q1 * bs, axis=1, keepdims=True)
    kj = lax.broadcasted_iota(jnp.int32, (rows, ne * cap), 1).astype(F32)
    s0 = (kj == f0).astype(BF)
    s1 = (kj == f1).astype(BF)
    zown.wait()
    for k in range(1, 16):
        c2, t2 = c ^ (k // 4), t ^ (k % 4)
        remote(zb.at[0], bb.at[c2 * 4 + t2], zsend.at[k], zrecv.at[k], c2, t2).wait_recv()
    for nb in range(4):
        cols = slice(nb * 512, (nb + 1) * 512)
        b = bb[:, :, cols].reshape(ne * cap, 512)
        z0 = jnp.dot(s0, b, preferred_element_type=F32)
        z1 = jnp.dot(s1, b, preferred_element_type=F32)
        acc = gates_ref[:, 0:1] * z0 + gates_ref[:, 1:2] * z1
        y_ref[:, cols] = (h_ref[:, cols].astype(F32) + acc).astype(BF)
    for cp in sends:
        cp.wait_send()


def params(cid):
    return pltpu.CompilerParams(collective_id=cid, has_side_effects=True, vmem_limit_bytes=60 * MIB)


def solution(mesh):
    rows_spec = P(('dp', 'cp', 'tp'), None)
    exp_spec = P(('cp', 'tp'), None, None)
    DMA = pltpu.SemaphoreType.DMA

    def local(x, idx, gates, wq, wk, wv, wo, w1g, w1u, w2):
        rows, d = x.shape
        seg = 2 * rows
        hc = wq.shape[1]
        ff = w1g.shape[2]
        sds = jax.ShapeDtypeStruct
        qkv, woa, cnt = pl.pallas_call(
            kernel_a, name='qkv_exchange',
            out_shape=(sds((3, 8, seg, HD), BF), sds((4, hc, d), BF), sds((16, 8, HD), F32)),
            in_specs=[VM, VM, VM, VM, VM, ANY], out_specs=(ANY, ANY, ANY),
            scratch_shapes=[
                pltpu.VMEM((4 * rows, d), BF), pltpu.VMEM((2, 3, 4, seg, HD), BF), pltpu.VMEM((8, HD), F32),
                DMA((3,)), DMA((4,)), DMA((3,)), DMA((4,)), DMA((2, 3, 4)), DMA((3, 8)), DMA((2, 3)), DMA((16,)), DMA((16,))],
            compiler_params=params(0))(x, idx, wq, wk, wv, wo)
        h = pl.pallas_call(
            kernel_b, name='attention',
            out_shape=sds((rows, d), BF),
            in_specs=[ANY, VM, ANY, ANY], out_specs=VM,
            scratch_shapes=[
                pltpu.VMEM((3, 8, seg, HD), BF), pltpu.VMEM((HD, 8 * seg), BF), pltpu.VMEM((4, hc, d), BF),
                pltpu.VMEM((HD, seg), F32), pltpu.VMEM((8, seg, HD), BF), pltpu.VMEM((rows, d), BF),
                DMA((3,)), DMA((4,)), DMA((8, 2)), DMA((1,)), DMA((16,))],
            compiler_params=params(1))(qkv, x, wo, woa)
        worst = jnp.max(cnt)

        def experts(cap, cid):
            def f(h, idx, idxt, gates, w1g, w1u, w2):
                return pl.pallas_call(
                    functools.partial(kernel_c, cap), name=f'experts{cap}',
                    out_shape=sds((rows, d), BF),
                    in_specs=[VM, VM, VM, VM, ANY, ANY, ANY], out_specs=VM,
                    scratch_shapes=[
                        pltpu.VMEM((d, ff), BF), pltpu.VMEM((d, ff), BF), pltpu.VMEM((ff, d), BF),
                        pltpu.VMEM((16, cap, d), BF), pltpu.VMEM((16, cap, d), BF), pltpu.VMEM((16, cap, d), BF), pltpu.VMEM((16, cap, d), BF),
                        DMA((3,)), DMA((16,)), DMA((16,)), DMA((16,)), DMA((16,)), DMA((1,)), DMA((1,))],
                    compiler_params=params(cid))(h, idx, idxt, gates, w1g, w1u, w2)
            return f

        caps = (32, 48, 64)
        which = (worst > caps[0]).astype(jnp.int32) + (worst > caps[1]).astype(jnp.int32)
        return lax.switch(which, [experts(cp, 2 + i) for i, cp in enumerate(caps)], h, idx, idx.T, gates, w1g, w1u, w2)

    return jax.shard_map(local, mesh=mesh, in_specs=(rows_spec, rows_spec, rows_spec, P(None, 'tp'), P(None, 'tp'), P(None, 'tp'), P('tp', None), exp_spec, exp_spec, exp_spec), out_specs=rows_spec, check_vma=False)
```

time: 781 us -> 353 us (0.45)
  waiting for transfers between devices: 332 us -> 0 us
  Pallas kernels: 0 us -> 321 us
  local copies, waits for them, and re-layouts: 171 us -> 4.06 us
  matrix products: 106 us -> 0 us
  blocking collectives: 99.2 us -> 0 us
  other arithmetic: 46.2 us -> 1.46 us
  loops' own time: 0 us -> 17.9 us
  between operations: 13.7 us -> 1.8 us
    pallas_call x0 -> x3, Pallas kernels: none -> 321 us  [the longest x1 200 us: f(): pl.pallas_call(functools.partial(kernel_c, cap), name=f'experts{cap}', ou...]
    all_gather x2 -> x0, waiting for transfers between devices: 175 us -> none  [the longest x1 139 us: attention_residual(): kvs = lax.all_gather(jnp.concatenate([k, v], axis=1), 'cp', axis=0)]
    dot_general x15 -> x0, matrix products: 106 us -> none  [the longest x4 45.5 us: attention_residual(): jnp.einsum('kgnm,mkd->kgnd', w.astype(jnp.bfloat16), vj, preferred_elemen...]
    all_to_all x1 -> x0, blocking collectives: 99.2 us -> none  [local(): recv = lax.all_to_all(send, ('cp', 'tp'), 0, 0, tiled=True)]
    scatter x1 -> x0, local copies, waits for them, and re-layouts: 92.8 us -> none  [local(): send = jnp.zeros((ne, cap, hd), jnp.bfloat16).at[ea, slot].set(h[tok])]
    all_to_all x1 -> x0, waiting for transfers between devices: 92.4 us -> none  [local(): lax.all_to_all(z.reshape(ne, cap, hd), ('cp', 'tp'), 0, 0, tiled=True)]
    reduce_scatter x1 -> x0, waiting for transfers between devices: 63.7 us -> none  [attention_residual(): att = lax.psum_scatter(part, 'tp', scatter_dimension=0, tiled=True)]
    reduce_sum x3 -> x0, other arithmetic: 35.5 us -> none  [the longest x2 26.6 us: attention_residual(): l = l * c + jnp.sum(w, axis=-1)]
  transfers between devices with their start and end apart: 4 -> 0, of which waited for: 4 -> 0; matrix products, arithmetic and copies ran while one was open for 2% -> 0% of each run, Pallas kernels for 0% -> 0%
where the time goes in v1:
time: 353 us; the launch traced here: 346 us
  Pallas kernels  321 us (91%)
  loops' own time  17.9 us (5%)
  local copies, waits for them, and re-layouts  4.06 us (1%)
    pallas_call x1, Pallas kernels, f(): pl.pallas_call(functools.partial(kernel_c, cap), name=f'experts{cap}', ou...  200 us
    pallas_call x1, Pallas kernels, local(): pl.pallas_call(kernel_a, name='qkv_exchange', out_shape=(sds((3, 8, seg,...  81.9 us
    pallas_call x1, Pallas kernels, local(): pl.pallas_call(kernel_b, name='attention', out_shape=sds((rows, d), BF),...  39.7 us
    another operation x1, loops' own time, local(): lax.switch(which, [experts(cp, 2 + i) for i, cp in enumerate(caps)], h, i...  17.9 us

profile of v1, /device:TPU:15, one launch (start us, length us, event | category | flops | bytes accessed | tf_op | source)
XLA Modules:
  0.0 346.5 jit_solution(14704198740115400385)
XLA Ops:
  0.0 1.5 copy.26.idx_ref
  1.5 81.9 %qkv_exchange.1 = (bf16[3,8,512,128]{3,2,1,0:T(8,128)(2,1)}, bf16[4,512,2048]{2,1,0:T(8,128)(2,1)}, f32[16,8,128]{2,1,0:T(8,128)}) custom-call(bf16[256,2048]{1,0:T(8,128)(2,1)} %x_ref.3, s32[256,2]{1,0:T(8,128)} %copy.26.idx_ref, bf16[2048,512]{1,0:T(8,128)(2,1)} %wq_ref.1, bf16[2048,512]{1,0:T(8,128)(2,1)} %wk_ref.1, bf16[2048,512]{1,0:T(8,128)(2,1)} %wv_ref.1, ...), custom_call_target="tpu_custom_call" | custom-call | tf_op jit(solution)/shard_map/qkv_exchange/pallas_call | solution.py:315
  83.4 1.5 reduce_max.9
  86.1 0.0 copy-start
  86.1 0.0 copy-start.1
  86.2 39.7 %attention.1 = bf16[256,2048]{1,0:T(8,128)(2,1)S(1)} custom-call(bf16[3,8,512,128]{3,2,1,0:T(8,128)(2,1)} %get-tuple-element.76.qkv_ref, bf16[256,2048]{1,0:T(8,128)(2,1)} %x_ref.3, bf16[512,2048]{1,0:T(8,128)(2,1)} %wo_ref.3, bf16[4,512,2048]{2,1,0:T(8,128)(2,1)} %get-tuple-element.77.woa_ref), custom_call_target="tpu_custom_call" | custom-call | tf_op jit(solution)/shard_map/attention/pallas_call | solution.py:323
  125.9 0.0 copy-done
  125.9 0.0 copy-done.1
  125.9 219.1 %conditional.1 = (bf16[256,2048]{1,0:T(8,128)(2,1)S(1)}) conditional(s32[]{:T(128)} %clamp.3, (bf16[256,2048]{1,0:T(8,128)(2,1)S(1)}, s32[256,2]{0,1:T(2,128)S(1)}, s32[2,256]{1,0:T(2,128)S(1)}, f32[256,2]{0,1:T(2,128)S(1)}, bf16[1,2048,1024]{2,1,0:T(8,128)(2,1)}, /*index=5*/bf16[1,2048,1024]{2,1,0:T(8,128)(2,1)}, ...), branch_computations={%region_1.0_spmd, %region_2.0_spmd, %region_3.0_spmd} | conditional | bytes 8200 | solution.py:349
  143.6 0.8 copy.32.gates_ref
  144.4 0.8 copy.31.idx_ref
  145.2 199.6 %experts64.1 = bf16[256,2048]{1,0:T(8,128)(2,1)S(1)} custom-call(bf16[256,2048]{1,0:T(8,128)(2,1)S(1)} %get-tuple-element.65.h_ref, s32[256,2]{1,0:T(8,128)} %copy.31.idx_ref, s32[2,256]{1,0:T(2,128)S(1)} %get-tuple-element.67.idxt_ref, f32[256,2]{1,0:T(8,128)} %copy.32.gates_ref, bf16[1,2048,1024]{2,1,0:T(8,128)(2,1)} %get-tuple-element.96.w1g_ref, ...), custom_call_target="tpu_custom_call" | custom-call | tf_op jit(solution)/shard_map/cond/branch_2_fun/experts64/pallas_call | solution.py:336
  345.0 1.0 copy.37
Async XLA Ops:
  86.1 39.8 %copy-start = (s32[256,2]{0,1:T(2,128)S(1)}, s32[256,2]{0,1:T(2,128)}, u32[]{:S(2)}) copy-start(s32[256,2]{0,1:T(2,128)} %param.14) | copy-start | bytes 6148
  86.1 39.8 %copy-start.1 = (f32[256,2]{0,1:T(2,128)S(1)}, f32[256,2]{0,1:T(2,128)}, u32[]{:S(2)}) copy-start(f32[256,2]{0,1:T(2,128)} %param.15) | copy-start | bytes 6148
